TPU v7x, 32 devices: a whole 2x2x4 slice. The times are simulated.
32 devices in a mesh: groups: 2 (over y), slab: 4 (over z), pencil: 2 (over x), comp: 2 (over core).
Axes of the slice: x: 2, y: 2, z: 4, core: 2. Of those that a mesh axis runs over, the one named last changes fastest.
Arguments:
- u_start: float32 [3, 64, 64, 512], P(None, ('groups', 'slab'), 'pencil', 'comp'), parts along dimension 1, may hold values from -6 to 6
- toughness: float32 [64, 64, 512], P(('groups', 'slab'), 'pencil', 'comp'), parts along dimension 0, may hold values from 0.3 to 1.5
- crack_label: int32 [64, 64, 512], P(('groups', 'slab'), 'pencil', 'comp'), parts along dimension 0, may hold values from 0 to 2
- obs_weight: bfloat16 [32, 64, 2, 4096], P('slab', 'pencil', 'comp'), may hold values from -0.75 to 0.75
- sensor_cell: int32 [4096], replicated, may hold values from 0 to 4095
Outputs:
- moved: float32 [3, 64, 64, 512], P(None, ('groups', 'slab'), 'pencil', 'comp'), parts along dimension 1
- damage: float32 [64, 64, 512], P(('groups', 'slab'), 'pencil', 'comp'), parts along dimension 0
- readings: float32 [3, 8192], P(None, 'groups'), parts along dimension 1
There are 2 independent parts, one for each index of `groups`. A program takes and returns all parts, laid end to end along the dimension named above; an argument that names none is the same for every part. Nothing has to cross between parts.
Inputs may be any that keep to these rules, and one draw needn't show every extreme that they name: `sensor_cell`: numbers cell blocks as (64 z + y) * 2 + h. `crack_label`: 0 intact, 1 partly cracked, 2 cracked.
All inputs are finite; a program needn't handle non-finite values.
Results may differ from a plain program's by a relative error of at most 0.003.
Values sent between devices are 32-bit elements; how exact they have to be, the bound alone decides.
A program may use at most 128 MiB of HBM per device.

v0:
```python
import jax
import jax.numpy as jnp
from jax import lax
from jax.sharding import PartitionSpec as P

SHEAR_MODULUS = 1.0
LAME_FIRST = 1.5
RESIDUAL_STIFF = 0.001
TIME_DISP = 0.15
TIME_DAMAGE = 0.08
LENGTH_SCALE = 1.0
DAMAGE_LEVEL = 0.45
POINT_GAIN = 8.0


def with_halo(block, sides, width):
    for axis, dim in sides:
        count = lax.axis_size(axis)
        forward = [(i, i + 1) for i in range(count - 1)]
        backward = [(target, source) for source, target in forward]
        low = lax.ppermute(
            lax.slice_in_dim(block, block.shape[dim] - width, None, axis=dim), axis, forward
        )
        high = lax.ppermute(lax.slice_in_dim(block, 0, width, axis=dim), axis, backward)
        block = jnp.concatenate([low, block, high], axis=dim)
    return block


def central(source, spatial):
    if spatial == 0:
        return 0.5 * (source[..., 2:, 1:-1, 1:-1] - source[..., :-2, 1:-1, 1:-1])
    if spatial == 1:
        return 0.5 * (source[..., 1:-1, 2:, 1:-1] - source[..., 1:-1, :-2, 1:-1])
    return 0.5 * (source[..., 1:-1, 1:-1, 2:] - source[..., 1:-1, 1:-1, :-2])


def shrink(source):
    return source[..., 1:-1, 1:-1, 1:-1]


def laplace(source):
    return (
        source[2:, 1:-1, 1:-1]
        + source[:-2, 1:-1, 1:-1]
        + source[1:-1, 2:, 1:-1]
        + source[1:-1, :-2, 1:-1]
        + source[1:-1, 1:-1, 2:]
        + source[1:-1, 1:-1, :-2]
        - 6.0 * source[1:-1, 1:-1, 1:-1]
    )


def entry_key(first, second):
    return (min(first, second), max(first, second))


def rotate(matrix, first, second):
    other = 3 - first - second
    diag_first = matrix[first, first]
    diag_second = matrix[second, second]
    coupling = matrix[first, second]
    angle = 0.5 * jnp.arctan2(2.0 * coupling, diag_second - diag_first)
    cosine = jnp.cos(angle)
    sine = jnp.sin(angle)
    side_first = matrix[entry_key(other, first)]
    side_second = matrix[entry_key(other, second)]
    result = dict(matrix)
    result[first, first] = (
        cosine * cosine * diag_first - 2.0 * cosine * sine * coupling + sine * sine * diag_second
    )
    result[second, second] = (
        sine * sine * diag_first + 2.0 * cosine * sine * coupling + cosine * cosine * diag_second
    )
    result[first, second] = jnp.zeros_like(coupling)
    result[entry_key(other, first)] = cosine * side_first - sine * side_second
    result[entry_key(other, second)] = sine * side_first + cosine * side_second
    return result


def eigenvalues(matrix):
    for sweep_index in range(5):
        for first, second in ((0, 1), (0, 2), (1, 2)):
            matrix = rotate(matrix, first, second)
    return [matrix[0, 0], matrix[1, 1], matrix[2, 2]]


def advance(padded_disp, padded_damage, toughness):
    gradient = [
        [central(padded_disp[component], direction) for direction in range(3)]
        for component in range(3)
    ]
    strain = {}
    for first in range(3):
        for second in range(first, 3):
            strain[first, second] = 0.5 * (gradient[first][second] + gradient[second][first])
    trace_full = strain[0, 0] + strain[1, 1] + strain[2, 2]
    damage_mid = shrink(padded_damage)
    degrade = (1.0 - damage_mid) ** 2 + RESIDUAL_STIFF
    divergence = []
    for component in range(3):
        total_force = 0.0
        for direction in range(3):
            stress = 2.0 * SHEAR_MODULUS * strain[entry_key(component, direction)]
            if component == direction:
                stress = stress + LAME_FIRST * trace_full
            total_force = total_force + central(degrade * stress, direction)
        divergence.append(total_force)
    moved = shrink(shrink(padded_disp)) + TIME_DISP * jnp.stack(divergence)
    inner = {key_pair: shrink(entry_value) for key_pair, entry_value in strain.items()}
    trace_inner = shrink(trace_full)
    energy = 0.5 * LAME_FIRST * jnp.maximum(trace_inner, 0.0) ** 2
    for eigen_value in eigenvalues(inner):
        energy = energy + SHEAR_MODULUS * jnp.maximum(eigen_value, 0.0) ** 2
    damage_core = shrink(damage_mid)
    damage = damage_core + TIME_DAMAGE * (
        2.0 * (1.0 - damage_core) * energy
        - toughness / LENGTH_SCALE * damage_core
        + toughness * LENGTH_SCALE * laplace(damage_mid)
    )
    return (moved, damage)


def local(u_start, toughness, crack_label, obs_weight, sensor_cell):
    planes, rows, columns = toughness.shape
    damage = DAMAGE_LEVEL * crack_label.astype(jnp.float32)
    moved = u_start
    for repeat in range(2):
        stacked = jnp.concatenate([moved, damage[None]], axis=0)
        padded = with_halo(stacked, (("slab", 1), ("pencil", 2), ("comp", 3)), 2)
        moved, damage = advance(padded[:3], padded[3], toughness)
    pooled = jnp.mean(moved, axis=-1).reshape(3, planes * rows).astype(jnp.bfloat16)
    weight_rows = obs_weight.reshape(planes * rows, obs_weight.shape[-1])
    dense = jnp.dot(pooled, weight_rows, preferred_element_type=jnp.float32)
    plane_ids = lax.axis_index("slab") * planes + jnp.arange(planes, dtype=jnp.int32)
    row_ids = lax.axis_index("pencil") * rows + jnp.arange(rows, dtype=jnp.int32)
    block_ids = (
        (plane_ids[:, None] * (rows * lax.axis_size("pencil")) + row_ids[None, :])
        * lax.axis_size("comp")
        + lax.axis_index("comp")
    ).reshape(planes * rows)
    picks = (block_ids[:, None] == sensor_cell[None, :]).astype(jnp.bfloat16)
    point = jnp.dot(pooled, picks, preferred_element_type=jnp.float32)
    partial_sum = dense + POINT_GAIN * point
    readings = lax.psum(partial_sum, ("slab", "pencil", "comp"))
    return (moved, damage, readings)


def solution(mesh):
    return jax.shard_map(
        local,
        mesh=mesh,
        in_specs=(
            P(None, ("groups", "slab"), "pencil", "comp"),
            P(("groups", "slab"), "pencil", "comp"),
            P(("groups", "slab"), "pencil", "comp"),
            P("slab", "pencil", "comp", None),
            P(),
        ),
        out_specs=(
            P(None, ("groups", "slab"), "pencil", "comp"),
            P(("groups", "slab"), "pencil", "comp"),
            P(None, "groups"),
        ),
        check_vma=False,
    )
```

profile of v0, /device:TPU:0, one launch (start us, length us, event | category | flops | bytes accessed | tf_op | source)
XLA Modules:
  0.0 226.6 jit_solution(18250146474018214217)
XLA Ops:
  0.6 0.0 copy-start
  0.6 0.0 copy-start.1
  0.7 1.1 multiply_bitcast_fusion
  1.8 1.1 pad_maximum_fusion.7
  2.9 5.0 %collective-permute-start = (f32[4,2,32,256]{3,2,1,0:T(8,128)S(1)}, f32[4,2,32,256]{3,2,1,0:T(8,128)S(1)}, u32[]{:S(2)}, u32[]{:S(2)}) collective-permute-start(f32[4,2,32,256]{3,2,1,0:T(8,128)S(1)} %get-tuple-element.66), channel_id=1, source_target_pairs={{0,4},{4,8},{8,12},{1,5},{5,9},{9,13},{2,6},{6,10},{10,14},{3,7},{... | collective-permute-start | bytes 786440 | tf_op jit(solution)/shard_map/ppermute | solution.py:21
  7.8 1.3 collective-permute-start.1
  9.1 4.2 %collective-permute-done = f32[4,2,32,256]{3,2,1,0:T(8,128)S(1)} collective-permute-done((f32[4,2,32,256]{3,2,1,0:T(8,128)S(1)}, f32[4,2,32,256]{3,2,1,0:T(8,128)S(1)}, u32[]{:S(2)}, u32[]{:S(2)}) %collective-permute-start) | collective-permute-done | bytes 262176 | tf_op jit(solution)/shard_map/ppermute | solution.py:21
  13.4 4.1 %collective-permute-done.1 = f32[4,2,32,256]{3,2,1,0:T(8,128)S(1)} collective-permute-done((f32[4,2,32,256]{3,2,1,0:T(8,128)S(1)}, f32[4,2,32,256]{3,2,1,0:T(8,128)S(1)}, u32[]{:S(2)}, u32[]{:S(2)}) %collective-permute-start.1) | collective-permute-done | bytes 262176 | tf_op jit(solution)/shard_map/ppermute | solution.py:24
  17.5 1.2 pad_maximum_fusion.15
  18.7 3.4 %collective-permute-start.2 = (f32[4,12,2,256]{3,2,1,0:T(2,128)S(1)}, f32[4,12,2,256]{3,2,1,0:T(2,128)S(1)}, u32[]{:S(2)}, u32[]{:S(2)}) collective-permute-start(f32[4,12,2,256]{3,2,1,0:T(2,128)S(1)} %get-tuple-element.58), channel_id=1, source_target_pairs={{0,2},{1,3},{4,6},{5,7},{8,10},{9,11},{12,14},{13,15},{16,18},{17,... | collective-permute-start | bytes 294920 | tf_op jit(solution)/shard_map/ppermute | solution.py:21
  22.1 1.3 collective-permute-start.3
  23.4 0.9 collective-permute-done.2
  24.3 4.3 %collective-permute-done.3 = f32[4,12,2,256]{3,2,1,0:T(2,128)S(1)} collective-permute-done((f32[4,12,2,256]{3,2,1,0:T(2,128)S(1)}, f32[4,12,2,256]{3,2,1,0:T(2,128)S(1)}, u32[]{:S(2)}, u32[]{:S(2)}) %collective-permute-start.3) | collective-permute-done | bytes 98336 | tf_op jit(solution)/shard_map/ppermute | solution.py:24
  28.6 0.3 pad_maximum_fusion.2
  28.9 1.6 fusion.80
  30.5 1.6 copy.24
  32.2 1.9 collective-permute-start.4
  34.1 2.2 copy.25
  36.3 1.3 collective-permute-start.5
  37.6 2.2 copy.26
  39.8 2.2 copy.27
  42.0 3.1 %pad_maximum_fusion = f32[4,12,36,260]{3,2,1,0:T(8,128)S(1)} fusion(f32[4,12,36,2]{3,2,1,0:T(8,128)} %copy.27, f32[4,12,2,256]{3,2,1,0:T(2,128)} %copy-done.13, f32[4,2,32,256]{3,2,1,0:T(8,128)} %copy-done.5, f32[1,8,32,256]{3,2,1,0:T(8,128)S(1)} %multiply_bitcast_fusion, f32[3,8,32,256]{3,2,1,0:T(8,128)S(1)} %copy-done.1, ...), kind=kLoop, calls=%fused_computation.3 | loop fusion | flops 3144960 | bytes 3594240 | tf_op jit(solution)/shard_map/concatenate | solution.py:25
  45.1 0.2 slice_bitcast_fusion.4
  45.3 2.2 multiply_multiply_fusion.5
  47.5 1.2 multiply_multiply_fusion.3
  48.8 0.0 copy-start.15
  48.8 1.1 fusion.69
  50.0 0.1 fusion.4
  50.1 0.0 copy-start.2
  50.1 29.3 %fusion.51 = f32[1,8,32,256]{3,2,1,0:T(8,128)S(1)} fusion(f32[8,32,256]{2,1,0:T(8,128)S(1)} %copy-done.15, f32[12,36,260]{2,1,0:T(8,128)S(1)} %get-tuple-element.37, f32[10,34,258]{2,1,0:T(8,128)S(1)} %get-tuple-element.46, f32[10,34,258]{2,1,0:T(8,128)S(1)} %get-tuple-element.47, f32[10,34,258]{2,1,0:T(8,128)S(1)} %get-tuple-element.29, ...), kind=kLoop, calls=%fused_computation.127 | loop fusion | flops 23068672 | bytes 4194304 | tf_op jit(solution)/shard_map/broadcast_in_dim | solution.py:128
  79.5 0.8 pad_maximum_fusion.5
  80.3 3.5 %collective-permute-start.6 = (f32[4,2,32,256]{3,2,1,0:T(8,128)}, f32[4,2,32,256]{3,2,1,0:T(8,128)S(1)}, u32[]{:S(2)}, u32[]{:S(2)}) collective-permute-start(f32[4,2,32,256]{3,2,1,0:T(8,128)} %get-tuple-element.64), channel_id=1, source_target_pairs={{0,4},{4,8},{8,12},{1,5},{5,9},{9,13},{2,6},{6,10},{10,14},{3,7},{... | collective-permute-start | bytes 786440 | tf_op jit(solution)/shard_map/ppermute | solution.py:21
  83.8 1.3 collective-permute-start.7
  85.1 0.6 add_multiply_fusion.6
  85.7 4.3 %collective-permute-done.6 = f32[4,2,32,256]{3,2,1,0:T(8,128)S(1)} collective-permute-done((f32[4,2,32,256]{3,2,1,0:T(8,128)}, f32[4,2,32,256]{3,2,1,0:T(8,128)S(1)}, u32[]{:S(2)}, u32[]{:S(2)}) %collective-permute-start.6) | collective-permute-done | bytes 262176 | tf_op jit(solution)/shard_map/ppermute | solution.py:21
  90.0 4.7 %collective-permute-done.7 = f32[4,2,32,256]{3,2,1,0:T(8,128)} collective-permute-done((f32[4,2,32,256]{3,2,1,0:T(8,128)}, f32[4,2,32,256]{3,2,1,0:T(8,128)}, u32[]{:S(2)}, u32[]{:S(2)}) %collective-permute-start.7) | collective-permute-done | bytes 262176 | tf_op jit(solution)/shard_map/ppermute | solution.py:24
  94.7 1.2 pad_maximum_fusion.11
  95.9 1.5 collective-permute-start.8
  97.4 1.3 collective-permute-start.9
  98.7 0.5 iota_add_fusion
  99.3 0.7 collective-permute-done.8
  100.0 4.1 %collective-permute-done.9 = f32[4,12,2,256]{3,2,1,0:T(2,128)S(1)} collective-permute-done((f32[4,12,2,256]{3,2,1,0:T(2,128)S(1)}, f32[4,12,2,256]{3,2,1,0:T(2,128)S(1)}, u32[]{:S(2)}, u32[]{:S(2)}) %collective-permute-start.9) | collective-permute-done | bytes 98336 | tf_op jit(solution)/shard_map/ppermute | solution.py:24
  104.1 1.5 pad_maximum_fusion.3
  105.6 1.6 fusion.79
  107.2 1.6 copy.28
  108.8 1.9 collective-permute-start.10
  110.7 2.2 copy.29
  113.0 1.3 collective-permute-start.11
  114.3 1.3 multiply_add_fusion.64
  115.6 1.3 add.757
  117.0 2.2 copy.30
  119.2 2.2 copy.31
  121.4 3.3 %pad_maximum_fusion.1 = f32[4,12,36,260]{3,2,1,0:T(8,128)S(1)} fusion(f32[4,12,36,2]{3,2,1,0:T(8,128)} %copy.31, f32[4,12,2,256]{3,2,1,0:T(2,128)} %copy-done.12, f32[4,2,32,256]{3,2,1,0:T(8,128)} %collective-permute-done.7, f32[1,8,32,256]{3,2,1,0:T(8,128)S(1)} %fusion.51, f32[3,8,32,256]{3,2,1,0:T(8,128)} %copy-done.2, ...), kind=kLoop, calls=%fused_computation.4 | loop fusion | flops 3144960 | bytes 3594240 | tf_op jit(solution)/shard_map/concatenate | solution.py:25
  124.7 0.2 slice_bitcast_fusion
  124.9 3.8 %multiply_multiply_fusion.2 = (f32[10,34,258]{2,1,0:T(8,128)S(1)}, f32[10,34,258]{2,1,0:T(8,128)}, f32[10,34,258]{2,1,0:T(8,128)S(1)}, f32[10,34,258]{2,1,0:T(8,...) fusion(f32[12,36,260]{2,1,0:T(8,128)S(1)} %get-tuple-element.33, ...), kind=kLoop, calls=%fused_computation.61 | loop fusion | flops 2456160 | bytes 8421120 | tf_op jit(solution)/shard_map/mul | solution.py:106
  128.7 2.1 multiply_multiply_fusion
  130.8 1.1 fusion.44
  132.0 0.0 copy-start.16
  132.0 1.1 fusion.71
  133.1 0.1 convert_element_type.19
  133.2 0.4 fusion.81
  133.6 1.4 fusion
  135.0 60.5 %psum.7 = f32[3,4096]{1,0:T(4,128)} all-reduce(f32[3,4096]{1,0:T(4,128)} %fusion), channel_id=1, replica_groups=mesh['groups'=2,'slab'=4,'pencil'=2,'comp'=2] {'slab','pencil','comp'}, use_global_device_ids=true, to_apply=%region_1.0 | all-reduce | flops 12288 | bytes 98304 | tf_op jit(solution)/shard_map/psum | solution.py:144
  195.5 31.0 %fusion.26 = f32[8,32,256]{2,1,0:T(8,128)} fusion(f32[8,32,256]{2,1,0:T(8,128)} %param.6, f32[12,36,260]{2,1,0:T(8,128)S(1)} %copy-done.4, f32[10,34,258]{2,1,0:T(8,128)S(1)} %get-tuple-element.39, f32[10,34,258]{2,1,0:T(8,128)} %get-tuple-element.40, f32[10,34,258]{2,1,0:T(8,128)} %get-tuple-element.18, f32[10,34,258]{2,1,0:T(8,128)} %get-tuple-element.44, ...), kind=kLoop, calls=%fused_computation.82 | loop fusion | flops 23068672 | bytes 4194304 | tf_op jit(solution)/shard_map/add | solution.py:115
  (34 shorter events, 0.1 us)
Async XLA Ops:
  0.6 132.5 %copy-start = (bf16[8,32,1,4096]{3,1,2,0:T(8,128)(2,1)S(1)}, bf16[8,32,1,4096]{3,1,2,0:T(8,128)(2,1)}, u32[]{:S(2)}) copy-start(bf16[8,32,1,4096]{3,1,2,0:T(8,128)(2,1)} %param.8) | copy-start | bytes 6291460
  0.6 28.0 %copy-start.1 = (f32[3,8,32,256]{3,2,1,0:T(8,128)S(1)}, f32[3,8,32,256]{3,2,1,0:T(8,128)}, u32[]{:S(2)}) copy-start(f32[3,8,32,256]{3,2,1,0:T(8,128)} %param.5) | copy-start | bytes 2359300
  2.9 10.5 %collective-permute-start = (f32[4,2,32,256]{3,2,1,0:T(8,128)S(1)}, f32[4,2,32,256]{3,2,1,0:T(8,128)S(1)}, u32[]{:S(2)}, u32[]{:S(2)}) collective-permute-start(f32[4,2,32,256]{3,2,1,0:T(8,128)S(1)} %get-tuple-element.66), channel_id=1, source_target_pairs={{0,4},{4,8},{8,12},{1,5},{5,9},{9,13},{2,6},{6,10},{10,14},{3,7},{... | collective-permute-start | bytes 786440 | tf_op jit(solution)/shard_map/ppermute | solution.py:21
  7.8 9.7 %collective-permute-start.1 = (f32[4,2,32,256]{3,2,1,0:T(8,128)S(1)}, f32[4,2,32,256]{3,2,1,0:T(8,128)S(1)}, u32[]{:S(2)}, u32[]{:S(2)}) collective-permute-start(f32[4,2,32,256]{3,2,1,0:T(8,128)S(1)} %get-tuple-element.67), channel_id=1, source_target_pairs={{4,0},{8,4},{12,8},{5,1},{9,5},{13,9},{6,2},{10,6},{14,10},{7,3},{... | collective-permute-start | bytes 786440 | tf_op jit(solution)/shard_map/ppermute | solution.py:24
  17.5 13.0 %copy-start.5 = (f32[4,2,32,256]{3,2,1,0:T(8,128)}, f32[4,2,32,256]{3,2,1,0:T(8,128)S(1)}, u32[]{:S(2)}) copy-start(f32[4,2,32,256]{3,2,1,0:T(8,128)S(1)} %collective-permute-done.1) | copy-start | bytes 786436
  18.7 5.6 %collective-permute-start.2 = (f32[4,12,2,256]{3,2,1,0:T(2,128)S(1)}, f32[4,12,2,256]{3,2,1,0:T(2,128)S(1)}, u32[]{:S(2)}, u32[]{:S(2)}) collective-permute-start(f32[4,12,2,256]{3,2,1,0:T(2,128)S(1)} %get-tuple-element.58), channel_id=1, source_target_pairs={{0,2},{1,3},{4,6},{5,7},{8,10},{9,11},{12,14},{13,15},{16,18},{17,... | collective-permute-start | bytes 294920 | tf_op jit(solution)/shard_map/ppermute | solution.py:21
  22.1 6.5 %collective-permute-start.3 = (f32[4,12,2,256]{3,2,1,0:T(2,128)S(1)}, f32[4,12,2,256]{3,2,1,0:T(2,128)S(1)}, u32[]{:S(2)}, u32[]{:S(2)}) collective-permute-start(f32[4,12,2,256]{3,2,1,0:T(2,128)S(1)} %get-tuple-element.59), channel_id=1, source_target_pairs={{2,0},{3,1},{6,4},{7,5},{10,8},{11,9},{14,12},{15,13},{18,16},{19,... | collective-permute-start | bytes 294920 | tf_op jit(solution)/shard_map/ppermute | solution.py:24
  28.6 1.9 copy-start.13
  32.2 5.4 %collective-permute-start.4 = (f32[4,12,36,2]{2,0,3,1:T(4,128)S(1)}, f32[4,12,36,2]{2,0,3,1:T(4,128)}, u32[]{:S(2)}, u32[]{:S(2)}) collective-permute-start(f32[4,12,36,2]{2,0,3,1:T(4,128)S(1)} %copy.24), channel_id=1, source_target_pairs={{0,1},{2,3},{4,5},{6,7},{8,9},{10,11},{12,13},{14,15},{16,17},{18,... | collective-permute-start | bytes 41480 | tf_op jit(solution)/shard_map/ppermute | solution.py:21
  36.3 3.5 %collective-permute-start.5 = (f32[4,12,36,2]{2,0,3,1:T(4,128)}, f32[4,12,36,2]{2,0,3,1:T(4,128)}, u32[]{:S(2)}, u32[]{:S(2)}) collective-permute-start(f32[4,12,36,2]{2,0,3,1:T(4,128)} %copy.25), channel_id=1, source_target_pairs={{1,0},{3,2},{5,4},{7,6},{9,8},{11,10},{13,12},{15,14},{17,16},{19,... | collective-permute-start | bytes 41480 | tf_op jit(solution)/shard_map/ppermute | solution.py:24
  48.8 1.3 copy-start.15
  49.9 29.5 %copy-start.6 = (f32[1,8,32,256]{3,2,1,0:T(8,128)}, f32[1,8,32,256]{3,2,1,0:T(8,128)S(1)}, u32[]{:S(2)}) copy-start(f32[1,8,32,256]{3,2,1,0:T(8,128)S(1)} %get-tuple-element.71) | copy-start | bytes 786436
  49.9 29.5 %copy-start.8 = (f32[1,8,32,256]{3,2,1,0:T(8,128)}, f32[1,8,32,256]{3,2,1,0:T(8,128)S(1)}, u32[]{:S(2)}) copy-start(f32[1,8,32,256]{3,2,1,0:T(8,128)S(1)} %get-tuple-element.72) | copy-start | bytes 786436
  50.0 29.5 %copy-start.10 = (f32[1,8,32,256]{3,2,1,0:T(8,128)}, f32[1,8,32,256]{3,2,1,0:T(8,128)S(1)}, u32[]{:S(2)}) copy-start(f32[1,8,32,256]{3,2,1,0:T(8,128)S(1)} %get-tuple-element.73) | copy-start | bytes 786436
  50.1 30.2 %copy-start.2 = (f32[3,8,32,256]{3,2,1,0:T(8,128)}, f32[3,8,32,256]{3,2,1,0:T(8,128)S(1)}, u32[]{:S(2)}) copy-start(f32[3,8,32,256]{3,2,1,0:T(8,128)S(1)} %fusion.4) | copy-start | bytes 2359300
  80.3 9.7 %collective-permute-start.6 = (f32[4,2,32,256]{3,2,1,0:T(8,128)}, f32[4,2,32,256]{3,2,1,0:T(8,128)S(1)}, u32[]{:S(2)}, u32[]{:S(2)}) collective-permute-start(f32[4,2,32,256]{3,2,1,0:T(8,128)} %get-tuple-element.64), channel_id=1, source_target_pairs={{0,4},{4,8},{8,12},{1,5},{5,9},{9,13},{2,6},{6,10},{10,14},{3,7},{... | collective-permute-start | bytes 786440 | tf_op jit(solution)/shard_map/ppermute | solution.py:21
  83.8 10.9 %collective-permute-start.7 = (f32[4,2,32,256]{3,2,1,0:T(8,128)}, f32[4,2,32,256]{3,2,1,0:T(8,128)}, u32[]{:S(2)}, u32[]{:S(2)}) collective-permute-start(f32[4,2,32,256]{3,2,1,0:T(8,128)} %get-tuple-element.65), channel_id=1, source_target_pairs={{4,0},{8,4},{12,8},{5,1},{9,5},{13,9},{6,2},{10,6},{14,10},{7,3},{... | collective-permute-start | bytes 786440 | tf_op jit(solution)/shard_map/ppermute | solution.py:24
  95.9 4.1 %collective-permute-start.8 = (f32[4,12,2,256]{3,2,1,0:T(2,128)S(1)}, f32[4,12,2,256]{3,2,1,0:T(2,128)S(1)}, u32[]{:S(2)}, u32[]{:S(2)}) collective-permute-start(f32[4,12,2,256]{3,2,1,0:T(2,128)S(1)} %get-tuple-element.56), channel_id=1, source_target_pairs={{0,2},{1,3},{4,6},{5,7},{8,10},{9,11},{12,14},{13,15},{16,18},{17,... | collective-permute-start | bytes 294920 | tf_op jit(solution)/shard_map/ppermute | solution.py:21
  97.4 6.7 %collective-permute-start.9 = (f32[4,12,2,256]{3,2,1,0:T(2,128)S(1)}, f32[4,12,2,256]{3,2,1,0:T(2,128)S(1)}, u32[]{:S(2)}, u32[]{:S(2)}) collective-permute-start(f32[4,12,2,256]{3,2,1,0:T(2,128)S(1)} %get-tuple-element.57), channel_id=1, source_target_pairs={{2,0},{3,1},{6,4},{7,5},{10,8},{11,9},{14,12},{15,13},{18,16},{19,... | collective-permute-start | bytes 294920 | tf_op jit(solution)/shard_map/ppermute | solution.py:24
  104.1 3.1 %copy-start.12 = (f32[4,12,2,256]{3,2,1,0:T(2,128)}, f32[4,12,2,256]{3,2,1,0:T(2,128)S(1)}, u32[]{:S(2)}) copy-start(f32[4,12,2,256]{3,2,1,0:T(2,128)S(1)} %collective-permute-done.9) | copy-start | bytes 294916
  108.8 8.1 %collective-permute-start.10 = (f32[4,12,36,2]{2,0,3,1:T(4,128)S(1)}, f32[4,12,36,2]{2,0,3,1:T(4,128)}, u32[]{:S(2)}, u32[]{:S(2)}) collective-permute-start(f32[4,12,36,2]{2,0,3,1:T(4,128)S(1)} %copy.28), channel_id=1, source_target_pairs={{0,1},{2,3},{4,5},{6,7},{8,9},{10,11},{12,13},{14,15},{16,17},{18,... | collective-permute-start | bytes 41480 | tf_op jit(solution)/shard_map/ppermute | solution.py:21
  113.0 6.2 %collective-permute-start.11 = (f32[4,12,36,2]{2,0,3,1:T(4,128)}, f32[4,12,36,2]{2,0,3,1:T(4,128)}, u32[]{:S(2)}, u32[]{:S(2)}) collective-permute-start(f32[4,12,36,2]{2,0,3,1:T(4,128)} %copy.29), channel_id=1, source_target_pairs={{1,0},{3,2},{5,4},{7,6},{9,8},{11,10},{13,12},{15,14},{17,16},{19,... | collective-permute-start | bytes 41480 | tf_op jit(solution)/shard_map/ppermute | solution.py:24
  124.9 3.8 %copy-start.3 = (f32[12,36,260]{2,1,0:T(8,128)}, f32[12,36,260]{2,1,0:T(8,128)S(1)}, u32[]{:S(2)}) copy-start(f32[12,36,260]{2,1,0:T(8,128)S(1)} %get-tuple-element.33) | copy-start | bytes 1347844
  130.8 1.2 copy-start.7
  130.8 1.2 copy-start.9
  130.8 1.2 copy-start.11
  132.0 1.6 copy-start.14
  132.0 1.6 copy-start.16
  133.1 62.5 %copy-start.4 = (f32[12,36,260]{2,1,0:T(8,128)S(1)}, f32[12,36,260]{2,1,0:T(8,128)}, u32[]{:S(2)}) copy-start(f32[12,36,260]{2,1,0:T(8,128)} %copy-done.3) | copy-start | bytes 1347844
where the time goes:
time: 228 us; the launch traced here: 227 us
  other arithmetic  89.2 us (39%)
  blocking collectives  60.5 us (27%)
  waiting for transfers between devices  27.4 us (12%)
  starting transfers between devices  24.9 us (11%)
  local copies, waits for them, and re-layouts  21.7 us (10%)
    psum x1, blocking collectives, local(): readings = lax.psum(partial_sum, ('slab', 'pencil', 'comp'))  60.5 us
    add x1, other arithmetic, advance(): damage_core + TIME_DAMAGE * (2.0 * (1.0 - damage_core) * energy - toughne...  31 us
    broadcast_in_dim x2, other arithmetic, local(): stacked = jnp.concatenate([moved, damage[None]], axis=0)  30.5 us
    ppermute x6, waiting for transfers between devices, with_halo(): lax.ppermute(lax.slice_in_dim(block, 0, width, axis=dim), axis, backward)  17.3 us
    ppermute x6, starting transfers between devices, with_halo(): lax.ppermute(lax.slice_in_dim(block, block.shape[dim] - width, None, axis...  17.2 us
    ppermute x6, waiting for transfers between devices, with_halo(): lax.ppermute(lax.slice_in_dim(block, block.shape[dim] - width, None, axis...  10.2 us
    mul x4, other arithmetic, advance(): total_force = total_force + central(degrade * stress, direction)  9.3 us
    concatenate x4, other arithmetic, with_halo(): block = jnp.concatenate([low, block, high], axis=dim)  8.23 us
  transfers between devices with their start and end apart: 12, of which 8 were waited for; matrix products, arithmetic and copies ran while one was open for 6% of the time, Pallas kernels for 0%

commit v1 on v0

--- a/solution.py
+++ b/solution.py
@@ -141,7 +141,8 @@
     picks = (block_ids[:, None] == sensor_cell[None, :]).astype(jnp.bfloat16)
     point = jnp.dot(pooled, picks, preferred_element_type=jnp.float32)
     partial_sum = dense + POINT_GAIN * point
-    readings = lax.psum(partial_sum, ("slab", "pencil", "comp"))
+    half = lax.psum(partial_sum, "slab")
+    readings = lax.psum(half, ("pencil", "comp"))
     return (moved, damage, readings)
 
 

time: 228 us -> 198 us (0.87)
  blocking collectives: 60.5 us -> 31 us
    psum x1 -> x2, blocking collectives: 60.5 us -> 31 us  [the longest x1 19 us: local(): half = lax.psum(partial_sum, 'slab')]
where the time goes in v1:
time: 198 us; the launch traced here: 197 us
  other arithmetic  89.2 us (45%)
  blocking collectives  31 us (16%)
  waiting for transfers between devices  27.4 us (14%)
  starting transfers between devices  24.9 us (13%)
  local copies, waits for them, and re-layouts  21.6 us (11%)
    add x1, other arithmetic, advance(): damage_core + TIME_DAMAGE * (2.0 * (1.0 - damage_core) * energy - toughne...  31 us
    broadcast_in_dim x2, other arithmetic, local(): stacked = jnp.concatenate([moved, damage[None]], axis=0)  30.5 us
    psum x1, blocking collectives, local(): half = lax.psum(partial_sum, 'slab')  19 us
    ppermute x6, waiting for transfers between devices, with_halo(): lax.ppermute(lax.slice_in_dim(block, 0, width, axis=dim), axis, backward)  17.3 us
    ppermute x6, starting transfers between devices, with_halo(): lax.ppermute(lax.slice_in_dim(block, block.shape[dim] - width, None, axis...  17.2 us
    psum x1, blocking collectives, local(): readings = lax.psum(half, ('pencil', 'comp'))  12 us
    ppermute x6, waiting for transfers between devices, with_halo(): lax.ppermute(lax.slice_in_dim(block, block.shape[dim] - width, None, axis...  10.2 us
    mul x4, other arithmetic, advance(): total_force = total_force + central(degrade * stress, direction)  9.29 us
  transfers between devices with their start and end apart: 12, of which 8 were waited for; matrix products, arithmetic and copies ran while one was open for 6% of the time, Pallas kernels for 0%

profile of v1, /device:TPU:0, one launch (start us, length us, event | category | flops | bytes accessed | tf_op | source)
XLA Modules:
  0.0 196.9 jit_solution(15091371741418481414)
XLA Ops:
  0.6 0.0 copy-start
  0.6 0.0 copy-start.1
  0.7 1.1 multiply_bitcast_fusion
  1.8 1.1 pad_maximum_fusion.7
  2.9 5.0 %collective-permute-start = (f32[4,2,32,256]{3,2,1,0:T(8,128)S(1)}, f32[4,2,32,256]{3,2,1,0:T(8,128)S(1)}, u32[]{:S(2)}, u32[]{:S(2)}) collective-permute-start(f32[4,2,32,256]{3,2,1,0:T(8,128)S(1)} %get-tuple-element.66), channel_id=1, source_target_pairs={{0,4},{4,8},{8,12},{1,5},{5,9},{9,13},{2,6},{6,10},{10,14},{3,7},{... | collective-permute-start | bytes 786440 | tf_op jit(solution)/shard_map/ppermute | solution.py:21
  7.8 1.3 collective-permute-start.1
  9.1 4.2 %collective-permute-done = f32[4,2,32,256]{3,2,1,0:T(8,128)S(1)} collective-permute-done((f32[4,2,32,256]{3,2,1,0:T(8,128)S(1)}, f32[4,2,32,256]{3,2,1,0:T(8,128)S(1)}, u32[]{:S(2)}, u32[]{:S(2)}) %collective-permute-start) | collective-permute-done | bytes 262176 | tf_op jit(solution)/shard_map/ppermute | solution.py:21
  13.4 4.1 %collective-permute-done.1 = f32[4,2,32,256]{3,2,1,0:T(8,128)S(1)} collective-permute-done((f32[4,2,32,256]{3,2,1,0:T(8,128)S(1)}, f32[4,2,32,256]{3,2,1,0:T(8,128)S(1)}, u32[]{:S(2)}, u32[]{:S(2)}) %collective-permute-start.1) | collective-permute-done | bytes 262176 | tf_op jit(solution)/shard_map/ppermute | solution.py:24
  17.5 1.2 pad_maximum_fusion.15
  18.7 3.4 %collective-permute-start.2 = (f32[4,12,2,256]{3,2,1,0:T(2,128)S(1)}, f32[4,12,2,256]{3,2,1,0:T(2,128)S(1)}, u32[]{:S(2)}, u32[]{:S(2)}) collective-permute-start(f32[4,12,2,256]{3,2,1,0:T(2,128)S(1)} %get-tuple-element.58), channel_id=1, source_target_pairs={{0,2},{1,3},{4,6},{5,7},{8,10},{9,11},{12,14},{13,15},{16,18},{17,... | collective-permute-start | bytes 294920 | tf_op jit(solution)/shard_map/ppermute | solution.py:21
  22.1 1.3 collective-permute-start.3
  23.4 0.9 collective-permute-done.2
  24.3 4.3 %collective-permute-done.3 = f32[4,12,2,256]{3,2,1,0:T(2,128)S(1)} collective-permute-done((f32[4,12,2,256]{3,2,1,0:T(2,128)S(1)}, f32[4,12,2,256]{3,2,1,0:T(2,128)S(1)}, u32[]{:S(2)}, u32[]{:S(2)}) %collective-permute-start.3) | collective-permute-done | bytes 98336 | tf_op jit(solution)/shard_map/ppermute | solution.py:24
  28.6 0.3 pad_maximum_fusion.2
  28.9 1.6 fusion.80
  30.5 1.6 copy.24
  32.1 1.9 collective-permute-start.4
  34.0 2.2 %copy.25 = f32[4,12,36,2]{2,0,3,1:T(4,128)} copy(f32[4,12,36,2]{3,2,1,0:T(8,128)} %get-tuple-element.55) | data formatting | bytes 27648 | tf_op jit(solution)/shard_map/slice | solution.py:24
  36.3 1.3 collective-permute-start.5
  37.6 2.2 %copy.26 = f32[4,12,36,2]{3,2,1,0:T(8,128)} copy(f32[4,12,36,2]{2,0,3,1:T(4,128)} %collective-permute-done.4) | data formatting | bytes 27648 | tf_op jit(solution)/shard_map/ppermute | solution.py:21
  39.8 2.2 %copy.27 = f32[4,12,36,2]{3,2,1,0:T(8,128)} copy(f32[4,12,36,2]{2,0,3,1:T(4,128)} %collective-permute-done.5) | data formatting | bytes 27648 | tf_op jit(solution)/shard_map/ppermute | solution.py:24
  42.0 3.1 %pad_maximum_fusion = f32[4,12,36,260]{3,2,1,0:T(8,128)S(1)} fusion(f32[4,12,36,2]{3,2,1,0:T(8,128)} %copy.27, f32[4,12,2,256]{3,2,1,0:T(2,128)} %copy-done.13, f32[4,2,32,256]{3,2,1,0:T(8,128)} %copy-done.5, f32[1,8,32,256]{3,2,1,0:T(8,128)S(1)} %multiply_bitcast_fusion, f32[3,8,32,256]{3,2,1,0:T(8,128)S(1)} %copy-done.1, ...), kind=kLoop, calls=%fused_computation.3 | loop fusion | flops 3144960 | bytes 3594240 | tf_op jit(solution)/shard_map/concatenate | solution.py:25
  45.1 0.2 slice_bitcast_fusion.4
  45.3 2.2 %multiply_multiply_fusion.5 = (f32[10,34,258]{2,1,0:T(8,128)S(1)}, f32[10,34,258]{2,1,0:T(8,128)S(1)}, f32[10,34,258]{2,1,0:T(8,128)S(1)}, f32[10,34,258]{2,1,0:...) fusion(f32[12,36,260]{2,1,0:T(8,128)S(1)} %get-tuple-element.37, ...), kind=kLoop, calls=%fused_computation.68 | loop fusion | flops 2456160 | bytes 8421120 | tf_op jit(solution)/shard_map/mul | solution.py:106
  47.5 1.2 multiply_multiply_fusion.3
  48.8 1.1 fusion.69
  49.9 0.1 fusion.4
  50.1 0.0 copy-start.2
  50.1 29.3 %fusion.51 = f32[1,8,32,256]{3,2,1,0:T(8,128)S(1)} fusion(f32[8,32,256]{2,1,0:T(8,128)S(1)} %copy-done.15, f32[12,36,260]{2,1,0:T(8,128)S(1)} %get-tuple-element.37, f32[10,34,258]{2,1,0:T(8,128)S(1)} %get-tuple-element.46, f32[10,34,258]{2,1,0:T(8,128)S(1)} %get-tuple-element.47, f32[10,34,258]{2,1,0:T(8,128)S(1)} %get-tuple-element.29, ...), kind=kLoop, calls=%fused_computation.127 | loop fusion | flops 23068672 | bytes 4194304 | tf_op jit(solution)/shard_map/broadcast_in_dim | solution.py:128
  79.5 0.8 pad_maximum_fusion.5
  80.3 3.5 %collective-permute-start.6 = (f32[4,2,32,256]{3,2,1,0:T(8,128)}, f32[4,2,32,256]{3,2,1,0:T(8,128)S(1)}, u32[]{:S(2)}, u32[]{:S(2)}) collective-permute-start(f32[4,2,32,256]{3,2,1,0:T(8,128)} %get-tuple-element.64), channel_id=1, source_target_pairs={{0,4},{4,8},{8,12},{1,5},{5,9},{9,13},{2,6},{6,10},{10,14},{3,7},{... | collective-permute-start | bytes 786440 | tf_op jit(solution)/shard_map/ppermute | solution.py:21
  83.8 1.3 collective-permute-start.7
  85.1 0.5 add_multiply_fusion.6
  85.6 4.4 %collective-permute-done.6 = f32[4,2,32,256]{3,2,1,0:T(8,128)S(1)} collective-permute-done((f32[4,2,32,256]{3,2,1,0:T(8,128)}, f32[4,2,32,256]{3,2,1,0:T(8,128)S(1)}, u32[]{:S(2)}, u32[]{:S(2)}) %collective-permute-start.6) | collective-permute-done | bytes 262176 | tf_op jit(solution)/shard_map/ppermute | solution.py:21
  90.0 4.7 %collective-permute-done.7 = f32[4,2,32,256]{3,2,1,0:T(8,128)} collective-permute-done((f32[4,2,32,256]{3,2,1,0:T(8,128)}, f32[4,2,32,256]{3,2,1,0:T(8,128)}, u32[]{:S(2)}, u32[]{:S(2)}) %collective-permute-start.7) | collective-permute-done | bytes 262176 | tf_op jit(solution)/shard_map/ppermute | solution.py:24
  94.7 1.2 pad_maximum_fusion.11
  95.8 1.5 collective-permute-start.8
  97.4 1.3 collective-permute-start.9
  98.7 0.6 iota_add_fusion
  99.3 0.7 collective-permute-done.8
  99.9 4.1 %collective-permute-done.9 = f32[4,12,2,256]{3,2,1,0:T(2,128)S(1)} collective-permute-done((f32[4,12,2,256]{3,2,1,0:T(2,128)S(1)}, f32[4,12,2,256]{3,2,1,0:T(2,128)S(1)}, u32[]{:S(2)}, u32[]{:S(2)}) %collective-permute-start.9) | collective-permute-done | bytes 98336 | tf_op jit(solution)/shard_map/ppermute | solution.py:24
  104.0 1.5 pad_maximum_fusion.3
  105.6 1.6 fusion.79
  107.2 1.6 copy.28
  108.8 1.9 collective-permute-start.10
  110.7 2.2 %copy.29 = f32[4,12,36,2]{2,0,3,1:T(4,128)} copy(f32[4,12,36,2]{3,2,1,0:T(8,128)} %get-tuple-element.53) | data formatting | bytes 27648 | tf_op jit(solution)/shard_map/slice | solution.py:24
  112.9 1.3 collective-permute-start.11
  114.2 1.3 multiply_add_fusion.64
  115.5 1.3 add.759
  116.8 2.2 %copy.30 = f32[4,12,36,2]{3,2,1,0:T(8,128)} copy(f32[4,12,36,2]{2,0,3,1:T(4,128)} %collective-permute-done.10) | data formatting | bytes 27648 | tf_op jit(solution)/shard_map/ppermute | solution.py:21
  119.1 2.2 %copy.31 = f32[4,12,36,2]{3,2,1,0:T(8,128)} copy(f32[4,12,36,2]{2,0,3,1:T(4,128)} %collective-permute-done.11) | data formatting | bytes 27648 | tf_op jit(solution)/shard_map/ppermute | solution.py:24
  121.2 3.3 %pad_maximum_fusion.1 = f32[4,12,36,260]{3,2,1,0:T(8,128)S(1)} fusion(f32[4,12,36,2]{3,2,1,0:T(8,128)} %copy.31, f32[4,12,2,256]{3,2,1,0:T(2,128)} %copy-done.12, f32[4,2,32,256]{3,2,1,0:T(8,128)} %collective-permute-done.7, f32[1,8,32,256]{3,2,1,0:T(8,128)S(1)} %fusion.51, f32[3,8,32,256]{3,2,1,0:T(8,128)} %copy-done.2, ...), kind=kLoop, calls=%fused_computation.4 | loop fusion | flops 3144960 | bytes 3594240 | tf_op jit(solution)/shard_map/concatenate | solution.py:25
  124.6 0.2 slice_bitcast_fusion
  124.8 3.8 %multiply_multiply_fusion.2 = (f32[10,34,258]{2,1,0:T(8,128)S(1)}, f32[10,34,258]{2,1,0:T(8,128)}, f32[10,34,258]{2,1,0:T(8,128)S(1)}, f32[10,34,258]{2,1,0:T(8,...) fusion(f32[12,36,260]{2,1,0:T(8,128)S(1)} %get-tuple-element.33, ...), kind=kLoop, calls=%fused_computation.61 | loop fusion | flops 2456160 | bytes 8421120 | tf_op jit(solution)/shard_map/mul | solution.py:106
  128.6 2.1 %multiply_multiply_fusion = (f32[10,34,258]{2,1,0:T(8,128)S(1)}, f32[10,34,258]{2,1,0:T(8,128)}, f32[10,34,258]{2,1,0:T(8,128)S(1)}, f32[10,34,258]{2,1,0:T(8,128)S(1)}) fusion(f32[12,36,260]{2,1,0:T(8,128)S(1)} %get-tuple-element.33, f32[12,36,260]{2,1,0:T(8,128)S(1)} %get-tuple-element.30, f32[12,36,260]{2,1,0:T(8,128)S(1)} %get-tuple-element.31, ...), kind=kLoop, calls=%fused_computation.58 | loop fusion | flops 1666680 | bytes 4912320 | tf_op jit(solution)/shard_map/mul | solution.py:106
  130.7 1.1 fusion.44
  131.8 0.0 copy-start.16
  131.9 1.1 fusion.71
  132.9 0.1 convert_element_type.19
  133.0 0.4 fusion.81
  133.4 1.4 fusion
  134.8 19.0 %psum.14 = f32[3,4096]{1,0:T(4,128)} all-reduce(f32[3,4096]{1,0:T(4,128)} %fusion), channel_id=1, replica_groups=mesh['groups'=2,'slab'=4,'pencil'=2,'comp'=2] {'slab'}, use_global_device_ids=true, to_apply=%region_1.0 | all-reduce | flops 12288 | bytes 98304 | tf_op jit(solution)/shard_map/psum | solution.py:144
  153.9 12.0 %psum.15 = f32[3,4096]{1,0:T(4,128)} all-reduce(f32[3,4096]{1,0:T(4,128)} %psum.14), channel_id=1, replica_groups=mesh['groups'=2,'slab'=4,'pencil'=2,'comp'=2] {'pencil','comp'}, use_global_device_ids=true, to_apply=%region_2.0 | all-reduce | flops 12288 | bytes 98304 | tf_op jit(solution)/shard_map/psum | solution.py:145
  165.8 31.0 %fusion.26 = f32[8,32,256]{2,1,0:T(8,128)} fusion(f32[8,32,256]{2,1,0:T(8,128)} %param.6, f32[12,36,260]{2,1,0:T(8,128)S(1)} %copy-done.4, f32[10,34,258]{2,1,0:T(8,128)S(1)} %get-tuple-element.39, f32[10,34,258]{2,1,0:T(8,128)} %get-tuple-element.40, f32[10,34,258]{2,1,0:T(8,128)} %get-tuple-element.18, f32[10,34,258]{2,1,0:T(8,128)} %get-tuple-element.44, ...), kind=kLoop, calls=%fused_computation.82 | loop fusion | flops 23068672 | bytes 4194304 | tf_op jit(solution)/shard_map/add | solution.py:115
  (35 shorter events, 0.1 us)
Async XLA Ops:
  0.6 132.4 %copy-start = (bf16[8,32,1,4096]{3,1,2,0:T(8,128)(2,1)S(1)}, bf16[8,32,1,4096]{3,1,2,0:T(8,128)(2,1)}, u32[]{:S(2)}) copy-start(bf16[8,32,1,4096]{3,1,2,0:T(8,128)(2,1)} %param.8) | copy-start | bytes 6291460
  0.6 28.0 %copy-start.1 = (f32[3,8,32,256]{3,2,1,0:T(8,128)S(1)}, f32[3,8,32,256]{3,2,1,0:T(8,128)}, u32[]{:S(2)}) copy-start(f32[3,8,32,256]{3,2,1,0:T(8,128)} %param.5) | copy-start | bytes 2359300
  2.9 10.5 %collective-permute-start = (f32[4,2,32,256]{3,2,1,0:T(8,128)S(1)}, f32[4,2,32,256]{3,2,1,0:T(8,128)S(1)}, u32[]{:S(2)}, u32[]{:S(2)}) collective-permute-start(f32[4,2,32,256]{3,2,1,0:T(8,128)S(1)} %get-tuple-element.66), channel_id=1, source_target_pairs={{0,4},{4,8},{8,12},{1,5},{5,9},{9,13},{2,6},{6,10},{10,14},{3,7},{... | collective-permute-start | bytes 786440 | tf_op jit(solution)/shard_map/ppermute | solution.py:21
  7.8 9.7 %collective-permute-start.1 = (f32[4,2,32,256]{3,2,1,0:T(8,128)S(1)}, f32[4,2,32,256]{3,2,1,0:T(8,128)S(1)}, u32[]{:S(2)}, u32[]{:S(2)}) collective-permute-start(f32[4,2,32,256]{3,2,1,0:T(8,128)S(1)} %get-tuple-element.67), channel_id=1, source_target_pairs={{4,0},{8,4},{12,8},{5,1},{9,5},{13,9},{6,2},{10,6},{14,10},{7,3},{... | collective-permute-start | bytes 786440 | tf_op jit(solution)/shard_map/ppermute | solution.py:24
  17.5 13.0 %copy-start.5 = (f32[4,2,32,256]{3,2,1,0:T(8,128)}, f32[4,2,32,256]{3,2,1,0:T(8,128)S(1)}, u32[]{:S(2)}) copy-start(f32[4,2,32,256]{3,2,1,0:T(8,128)S(1)} %collective-permute-done.1) | copy-start | bytes 786436
  18.7 5.6 %collective-permute-start.2 = (f32[4,12,2,256]{3,2,1,0:T(2,128)S(1)}, f32[4,12,2,256]{3,2,1,0:T(2,128)S(1)}, u32[]{:S(2)}, u32[]{:S(2)}) collective-permute-start(f32[4,12,2,256]{3,2,1,0:T(2,128)S(1)} %get-tuple-element.58), channel_id=1, source_target_pairs={{0,2},{1,3},{4,6},{5,7},{8,10},{9,11},{12,14},{13,15},{16,18},{17,... | collective-permute-start | bytes 294920 | tf_op jit(solution)/shard_map/ppermute | solution.py:21
  22.1 6.5 %collective-permute-start.3 = (f32[4,12,2,256]{3,2,1,0:T(2,128)S(1)}, f32[4,12,2,256]{3,2,1,0:T(2,128)S(1)}, u32[]{:S(2)}, u32[]{:S(2)}) collective-permute-start(f32[4,12,2,256]{3,2,1,0:T(2,128)S(1)} %get-tuple-element.59), channel_id=1, source_target_pairs={{2,0},{3,1},{6,4},{7,5},{10,8},{11,9},{14,12},{15,13},{18,16},{19,... | collective-permute-start | bytes 294920 | tf_op jit(solution)/shard_map/ppermute | solution.py:24
  28.6 1.9 copy-start.13
  32.1 5.4 %collective-permute-start.4 = (f32[4,12,36,2]{2,0,3,1:T(4,128)S(1)}, f32[4,12,36,2]{2,0,3,1:T(4,128)}, u32[]{:S(2)}, u32[]{:S(2)}) collective-permute-start(f32[4,12,36,2]{2,0,3,1:T(4,128)S(1)} %copy.24), channel_id=1, source_target_pairs={{0,1},{2,3},{4,5},{6,7},{8,9},{10,11},{12,13},{14,15},{16,17},{18,... | collective-permute-start | bytes 41480 | tf_op jit(solution)/shard_map/ppermute | solution.py:21
  36.3 3.5 %collective-permute-start.5 = (f32[4,12,36,2]{2,0,3,1:T(4,128)}, f32[4,12,36,2]{2,0,3,1:T(4,128)}, u32[]{:S(2)}, u32[]{:S(2)}) collective-permute-start(f32[4,12,36,2]{2,0,3,1:T(4,128)} %copy.25), channel_id=1, source_target_pairs={{1,0},{3,2},{5,4},{7,6},{9,8},{11,10},{13,12},{15,14},{17,16},{19,... | collective-permute-start | bytes 41480 | tf_op jit(solution)/shard_map/ppermute | solution.py:24
  48.7 1.3 copy-start.15
  49.9 29.5 %copy-start.6 = (f32[1,8,32,256]{3,2,1,0:T(8,128)}, f32[1,8,32,256]{3,2,1,0:T(8,128)S(1)}, u32[]{:S(2)}) copy-start(f32[1,8,32,256]{3,2,1,0:T(8,128)S(1)} %get-tuple-element.71) | copy-start | bytes 786436
  49.9 29.5 %copy-start.8 = (f32[1,8,32,256]{3,2,1,0:T(8,128)}, f32[1,8,32,256]{3,2,1,0:T(8,128)S(1)}, u32[]{:S(2)}) copy-start(f32[1,8,32,256]{3,2,1,0:T(8,128)S(1)} %get-tuple-element.72) | copy-start | bytes 786436
  49.9 29.5 %copy-start.10 = (f32[1,8,32,256]{3,2,1,0:T(8,128)}, f32[1,8,32,256]{3,2,1,0:T(8,128)S(1)}, u32[]{:S(2)}) copy-start(f32[1,8,32,256]{3,2,1,0:T(8,128)S(1)} %get-tuple-element.73) | copy-start | bytes 786436
  50.1 30.2 %copy-start.2 = (f32[3,8,32,256]{3,2,1,0:T(8,128)}, f32[3,8,32,256]{3,2,1,0:T(8,128)S(1)}, u32[]{:S(2)}) copy-start(f32[3,8,32,256]{3,2,1,0:T(8,128)S(1)} %fusion.4) | copy-start | bytes 2359300
  80.3 9.7 %collective-permute-start.6 = (f32[4,2,32,256]{3,2,1,0:T(8,128)}, f32[4,2,32,256]{3,2,1,0:T(8,128)S(1)}, u32[]{:S(2)}, u32[]{:S(2)}) collective-permute-start(f32[4,2,32,256]{3,2,1,0:T(8,128)} %get-tuple-element.64), channel_id=1, source_target_pairs={{0,4},{4,8},{8,12},{1,5},{5,9},{9,13},{2,6},{6,10},{10,14},{3,7},{... | collective-permute-start | bytes 786440 | tf_op jit(solution)/shard_map/ppermute | solution.py:21
  83.8 10.9 %collective-permute-start.7 = (f32[4,2,32,256]{3,2,1,0:T(8,128)}, f32[4,2,32,256]{3,2,1,0:T(8,128)}, u32[]{:S(2)}, u32[]{:S(2)}) collective-permute-start(f32[4,2,32,256]{3,2,1,0:T(8,128)} %get-tuple-element.65), channel_id=1, source_target_pairs={{4,0},{8,4},{12,8},{5,1},{9,5},{13,9},{6,2},{10,6},{14,10},{7,3},{... | collective-permute-start | bytes 786440 | tf_op jit(solution)/shard_map/ppermute | solution.py:24
  95.8 4.1 %collective-permute-start.8 = (f32[4,12,2,256]{3,2,1,0:T(2,128)S(1)}, f32[4,12,2,256]{3,2,1,0:T(2,128)S(1)}, u32[]{:S(2)}, u32[]{:S(2)}) collective-permute-start(f32[4,12,2,256]{3,2,1,0:T(2,128)S(1)} %get-tuple-element.56), channel_id=1, source_target_pairs={{0,2},{1,3},{4,6},{5,7},{8,10},{9,11},{12,14},{13,15},{16,18},{17,... | collective-permute-start | bytes 294920 | tf_op jit(solution)/shard_map/ppermute | solution.py:21
  97.4 6.7 %collective-permute-start.9 = (f32[4,12,2,256]{3,2,1,0:T(2,128)S(1)}, f32[4,12,2,256]{3,2,1,0:T(2,128)S(1)}, u32[]{:S(2)}, u32[]{:S(2)}) collective-permute-start(f32[4,12,2,256]{3,2,1,0:T(2,128)S(1)} %get-tuple-element.57), channel_id=1, source_target_pairs={{2,0},{3,1},{6,4},{7,5},{10,8},{11,9},{14,12},{15,13},{18,16},{19,... | collective-permute-start | bytes 294920 | tf_op jit(solution)/shard_map/ppermute | solution.py:24
  104.0 3.1 %copy-start.12 = (f32[4,12,2,256]{3,2,1,0:T(2,128)}, f32[4,12,2,256]{3,2,1,0:T(2,128)S(1)}, u32[]{:S(2)}) copy-start(f32[4,12,2,256]{3,2,1,0:T(2,128)S(1)} %collective-permute-done.9) | copy-start | bytes 294916
  108.8 8.1 %collective-permute-start.10 = (f32[4,12,36,2]{2,0,3,1:T(4,128)S(1)}, f32[4,12,36,2]{2,0,3,1:T(4,128)}, u32[]{:S(2)}, u32[]{:S(2)}) collective-permute-start(f32[4,12,36,2]{2,0,3,1:T(4,128)S(1)} %copy.28), channel_id=1, source_target_pairs={{0,1},{2,3},{4,5},{6,7},{8,9},{10,11},{12,13},{14,15},{16,17},{18,... | collective-permute-start | bytes 41480 | tf_op jit(solution)/shard_map/ppermute | solution.py:21
  112.9 6.1 %collective-permute-start.11 = (f32[4,12,36,2]{2,0,3,1:T(4,128)}, f32[4,12,36,2]{2,0,3,1:T(4,128)}, u32[]{:S(2)}, u32[]{:S(2)}) collective-permute-start(f32[4,12,36,2]{2,0,3,1:T(4,128)} %copy.29), channel_id=1, source_target_pairs={{1,0},{3,2},{5,4},{7,6},{9,8},{11,10},{13,12},{15,14},{17,16},{19,... | collective-permute-start | bytes 41480 | tf_op jit(solution)/shard_map/ppermute | solution.py:24
  124.8 3.8 %copy-start.3 = (f32[12,36,260]{2,1,0:T(8,128)}, f32[12,36,260]{2,1,0:T(8,128)S(1)}, u32[]{:S(2)}) copy-start(f32[12,36,260]{2,1,0:T(8,128)S(1)} %get-tuple-element.33) | copy-start | bytes 1347844
  130.7 1.2 copy-start.7
  130.7 1.2 copy-start.9
  130.7 1.2 copy-start.11
  131.8 1.6 copy-start.14
  131.8 1.6 copy-start.16
  132.9 32.9 %copy-start.4 = (f32[12,36,260]{2,1,0:T(8,128)S(1)}, f32[12,36,260]{2,1,0:T(8,128)}, u32[]{:S(2)}) copy-start(f32[12,36,260]{2,1,0:T(8,128)} %copy-done.3) | copy-start | bytes 1347844
